TPU v7x, 32 devices: a whole 2x2x4 slice. The times are simulated.
32 devices in a mesh: seq: 4 (over y, x), fsdp: 8 (over z, core).
Axes of the slice: x: 2, y: 2, z: 4, core: 2. Of those that a mesh axis runs over, the one named last changes fastest.
Arguments:
- tokens: bfloat16 [8, 512, 8192], P('fsdp', 'seq'), may hold values from -6 to 6
- norm_gain: float32 [8192], replicated, may hold values from 0.3 to 3
- w_query: bfloat16 [8192, 4096], P(('seq', 'fsdp')), may hold values from -1 to 1
- key_weight: bfloat16 [8192, 512], P(('seq', 'fsdp')), may hold values from -1 to 1
- value_weight: bfloat16 [8192, 512], P(('seq', 'fsdp')), may hold values from -0.0625 to 0.0625
- w_out: bfloat16 [4096, 8192], P(None, ('seq', 'fsdp')), may hold values from -0.09375 to 0.09375
Outputs:
- result: float32 [8, 512, 8192], P('fsdp', 'seq')
All inputs are finite; a program needn't handle non-finite values.
Results may differ from a plain program's by a relative error of at most 0.04.
Values may be sent and summed in bfloat16 or wider, within the bound.
A program may use at most 128 MiB of HBM per device.

v0:
```python
import jax
import jax.numpy as jnp
from jax import lax
from jax.sharding import PartitionSpec as P

HEAD_SIZE = 128


def body(tokens, norm_gain, w_query, key_weight, value_weight, w_out):
    floats = tokens[0].astype(jnp.float32)
    mean_square = jnp.mean(floats * floats, axis=-1, keepdims=True)
    normed_input = (floats * lax.rsqrt(mean_square + 1e-05) * norm_gain).astype(jnp.bfloat16)
    spread = lax.all_to_all(normed_input[None], "seq", split_axis=2, concat_axis=1, tiled=True)[0]
    seq_length = spread.shape[0]
    group_size = lax.axis_size("seq")
    device_index = lax.axis_index("seq")
    query_heads = w_query.shape[1] // HEAD_SIZE
    key_heads = key_weight.shape[1] // HEAD_SIZE
    group_width = query_heads // key_heads
    local_heads = query_heads // group_size
    portions = (
        lax.all_gather(w_query, "fsdp", axis=0, tiled=True),
        lax.all_gather(key_weight, "fsdp", axis=0, tiled=True),
        lax.all_gather(value_weight, "fsdp", axis=0, tiled=True),
    )
    query_part, key_part, value_part = tuple(
        (jnp.dot(spread, portion, preferred_element_type=jnp.float32) for portion in portions)
    )
    query_sum = lax.psum_scatter(
        query_part.astype(jnp.bfloat16), "seq", scatter_dimension=1, tiled=True
    )
    key_all, value_all = (
        lax.psum(key_part.astype(jnp.bfloat16), "seq").astype(jnp.float32),
        lax.psum(value_part.astype(jnp.bfloat16), "seq").astype(jnp.float32),
    )
    offset = device_index * local_heads // group_width * HEAD_SIZE
    key_rows = lax.dynamic_slice_in_dim(key_all, offset, HEAD_SIZE, 1).astype(jnp.bfloat16)
    value_rows = lax.dynamic_slice_in_dim(value_all, offset, HEAD_SIZE, 1).astype(jnp.bfloat16)
    queries = jnp.transpose(query_sum.reshape(seq_length, local_heads, HEAD_SIZE), (1, 0, 2))
    scale = HEAD_SIZE ** (-0.5)
    row_ids = lax.broadcasted_iota(jnp.int32, (seq_length, seq_length), 0)
    col_ids = lax.broadcasted_iota(jnp.int32, (seq_length, seq_length), 1)
    causal = row_ids >= col_ids

    def one_head(query_head):
        scores = (
            jnp.einsum("qd,kd->qk", query_head, key_rows, preferred_element_type=jnp.float32)
            * scale
        )
        scores = jnp.where(causal, scores, jnp.float32(-1e30))
        top = jnp.max(scores, axis=-1, keepdims=True)
        weights = jnp.exp(scores - top)
        probs = (weights / jnp.sum(weights, axis=-1, keepdims=True)).astype(jnp.bfloat16)
        return jnp.dot(probs, value_rows, preferred_element_type=jnp.float32).astype(jnp.bfloat16)

    attended = lax.map(one_head, queries)
    heads_out = jnp.transpose(attended, (1, 0, 2)).reshape(seq_length, local_heads * HEAD_SIZE)
    out_columns = lax.all_gather(w_out, "fsdp", axis=1, tiled=True)
    mixed = jnp.dot(
        lax.all_gather(heads_out, "seq", axis=1, tiled=True),
        out_columns,
        preferred_element_type=jnp.float32,
    )
    branch = mixed.astype(jnp.bfloat16)
    returned = lax.all_to_all(branch[None], "seq", split_axis=1, concat_axis=2, tiled=True)
    return tokens.astype(jnp.float32) + returned.astype(jnp.float32)


def solution(mesh):
    placed = (
        P("fsdp", "seq", None),
        P(),
        P(("seq", "fsdp"), None),
        P(("seq", "fsdp"), None),
        P(("seq", "fsdp"), None),
        P(None, ("seq", "fsdp")),
    )
    return jax.shard_map(
        body, mesh=mesh, in_specs=placed, out_specs=P("fsdp", "seq", None), check_vma=False
    )
```

profile of v0, /device:TPU:0, one launch (start us, length us, event | category | flops | bytes accessed | tf_op | source)
XLA Modules:
  0.0 635.2 jit_solution(5943152748968882074)
XLA Ops:
  11.2 9.5 %copy.25 = bf16[1,128,8192]{1,0,2:T(2,128)(2,1)} copy(bf16[1,128,8192]{2,1,0:T(8,128)(2,1)} %fusion.10) | data formatting | bytes 4194304 | tf_op jit(solution)/shard_map/convert_element_type | solution.py:12
  21.3 46.5 %reduce.1 = bf16[8192,128]{1,0:T(8,128)(2,1)} reduce(bf16[8192,1,128]{2,1,0:T(2,128)(2,1)} %bitcast.52, bf16[]{:T(256)} %broadcast.27), dimensions={1}, to_apply=%bitcast.23.reduce_sub_computation | reduce | bytes 4194306
  67.8 4.0 reshape.53
  71.8 31.4 %all_to_all.24 = bf16[4,2,131072]{2,1,0:T(2,128)(2,1)} all-to-all(bf16[4,2,131072]{2,1,0:T(2,128)(2,1)} %reshape.53), channel_id=1, replica_groups=mesh['seq'=4,'fsdp'=8] {'seq'}, dimensions={0} | all-to-all | bytes 4194304 | tf_op jit(solution)/shard_map/all_to_all | solution.py:13
  103.2 4.9 reshape.54
  112.0 4.0 copy.26
  116.0 4.3 convolution_convert_fusion.3
  120.3 4.4 convolution_convert_fusion.4
  125.0 98.2 %all-gather.6.cloned.1.call-done = bf16[2048,4096]{1,0:T(8,128)(2,1)} async-done(((bf16[256,4096]{1,0:T(8,128)(2,1)}), bf16[2048,4096]{1,0:T(8,128)(2,1)}) %all-gather.6.cloned.1.call-update) | async-done | bytes 16777232 | tf_op jit(solution)/shard_map/all_gather | solution.py:22
  223.1 14.3 %convolution_convert_fusion.1 = bf16[512,4096]{1,0:T(8,128)(2,1)} fusion(bf16[512,2048]{1,0:T(8,128)(2,1)} %bitcast.60, bf16[2048,4096]{1,0:T(8,128)(2,1)} %all-gather.6.cloned.1.call-done), kind=kOutput, calls=%fused_computation.16 | convolution fusion | flops 8592031744 | bytes 23068672 | tf_op jit(solution)/shard_map/dot_general | solution.py:27
  238.1 38.6 %all-reduce.3.cloned.1.call-done = (bf16[512,512]{1,0:T(8,128)(2,1)}, bf16[512,512]{1,0:T(8,128)(2,1)}) async-done(((bf16[512,512]{1,0:T(8,128)(2,1)}, bf16[512,512]{1,0:T(8,128)(2,1)}), (bf16[512,512]{1,0:T(8,128)(2,1)}, bf16[512,512]{1,0:T(8,128)(2,1)})) %all-reduce.3.cloned.1.call-update) | async-done | bytes 1048592 | tf_op jit(solution)/shard_map/psum | solution.py:33
  278.4 53.8 %reduce-scatter.2.cloned.1.call-done = bf16[512,1024]{1,0:T(8,128)(2,1)} async-done(((bf16[512,4096]{1,0:T(8,128)(2,1)}), bf16[512,1024]{1,0:T(8,128)(2,1)}) %reduce-scatter.2.cloned.1.call-update) | async-done | bytes 1048592 | tf_op jit(solution)/shard_map/reduce_scatter | solution.py:29
  334.6 16.4 %while.11 = (s32[]{:T(128)}, bf16[8,512,128]{1,2,0:T(8,128)(2,1)S(1)}, bf16[8,512,128]{2,1,0:T(8,128)(2,1)}, bf16[512,128]{1,0:T(8,128)(2,1)}, bf16[512,128]{1,0:T(8,128)(2,1)S(1)}, /*index=5*/s32[]{:T(128)}) while((s32[]{:T(128)}, bf16[8,512,128]{1,2,0:T(8,128)(2,1)S(1)}, bf16[8,512,128]{2,1,0:T(8,128)(2,1)}, ...), condition=%wide.region_7.8_spmd.clone, body=%wide.region_4.7_spmd.clone.sunk | while | flops 136641536 | bytes 4205129 | solution.py:56
  351.9 133.5 %all-gather.14.cloned.1.call-done = bf16[4096,2048]{1,0:T(8,128)(2,1)} async-done(((bf16[4096,256]{1,0:T(8,128)(2,1)}), bf16[4096,2048]{1,0:T(8,128)(2,1)}) %all-gather.14.cloned.1.call-update) | async-done | bytes 16777232 | tf_op jit(solution)/shard_map/all_gather | solution.py:58
  485.5 52.6 %all-gather.12.cloned.1.call-done = bf16[512,4096]{0,1:T(8,128)(2,1)} async-done(((bf16[512,1024]{0,1:T(8,128)(2,1)}), bf16[512,4096]{0,1:T(8,128)(2,1)}) %all-gather.12.cloned.1.call-update) | async-done | bytes 4194320 | tf_op jit(solution)/shard_map/all_gather | solution.py:60
  538.1 13.6 %fusion.11 = bf16[1,512,2048]{2,1,0:T(8,128)(2,1)S(1)} fusion(bf16[512,4096]{0,1:T(8,128)(2,1)} %all-gather.12.cloned.1.call-done, bf16[4096,2048]{1,0:T(8,128)(2,1)} %all-gather.14.cloned.1.call-done), kind=kOutput, calls=%fused_computation.22 | convolution fusion | flops 8590983168 | bytes 23068672 | tf_op jit(solution)/shard_map/dot_general | solution.py:59
  551.7 5.2 copy.39
  557.0 14.5 %reduce.2 = bf16[512,2048]{1,0:T(8,128)(2,1)} reduce(bf16[512,1,2048]{2,1,0:T(2,128)(2,1)} %bitcast.53, bf16[]{:T(256)} %broadcast.27), dimensions={1}, to_apply=%bitcast.43.reduce_sub_computation | reduce | bytes 4194306
  571.5 4.5 reshape.55
  576.0 29.9 %all_to_all.25 = bf16[4,2,131072]{2,1,0:T(2,128)(2,1)} all-to-all(bf16[4,2,131072]{2,1,0:T(2,128)(2,1)} %reshape.55), channel_id=1, replica_groups=mesh['seq'=4,'fsdp'=8] {'seq'}, dimensions={0} | all-to-all | bytes 4194304 | tf_op jit(solution)/shard_map/all_to_all | solution.py:65
  605.9 4.9 reshape.56
  610.9 6.8 %copy.38 = f32[1,4,128,2048]{3,1,2,0:T(4,128)} copy(bf16[1,4,128,2048]{3,0,2,1:T(2,128)(2,1)} %bitcast.55) | data formatting | bytes 6291456 | tf_op jit(solution)/shard_map/convert_element_type | solution.py:66
  617.7 6.0 reshape.51
  623.7 4.6 convert_add_fusion
  (70 shorter events, 31.0 us)
Async XLA Ops:
  6.5 2.3 copy-start
  6.5 109.5 %all-gather.10.cloned.1.call-start = ((), (), s32[]{:S(2)}) async-start(), calls=%async_computation.6 | async-start | bytes 2359296 | tf_op jit(solution)/shard_map/all_gather | solution.py:24
  7.3 113.0 %all-gather.8.cloned.1.call-start = ((), (), s32[]{:S(2)}) async-start(), calls=%async_computation.5 | async-start | bytes 2359296 | tf_op jit(solution)/shard_map/all_gather | solution.py:23
  8.0 1.3 copy-start.2
  8.0 215.1 %all-gather.6.cloned.1.call-start = ((), (), s32[]{:S(2)}) async-start(), calls=%async_computation.3 | async-start | bytes 18874368 | tf_op jit(solution)/shard_map/all_gather | solution.py:22
  8.8 268.0 %all-reduce.3.cloned.1.call-start = ((), (), s32[]{:S(2)}) async-start(), calls=%async_computation.9 | async-start | bytes 2097152 | tf_op jit(solution)/shard_map/psum | solution.py:33
  124.7 207.4 %reduce-scatter.2.cloned.1.call-start = ((), (), s32[]{:S(2)}) async-start(), calls=%async_computation.4 | async-start | bytes 5242880 | tf_op jit(solution)/shard_map/reduce_scatter | solution.py:29
  237.5 248.0 %all-gather.14.cloned.1.call-start = ((), (), s32[]{:S(2)}) async-start(), calls=%async_computation.8 | async-start | bytes 18874368 | tf_op jit(solution)/shard_map/all_gather | solution.py:58
  238.0 300.0 %all-gather.12.cloned.1.call-start = ((), (), s32[]{:S(2)}) async-start(), calls=%async_computation.7 | async-start | bytes 5242880 | tf_op jit(solution)/shard_map/all_gather | solution.py:60
  350.9 1.0 copy-start.1
Sparse Core Ops, SparseCore 0:
  8.9 31.8 all-gather.9
  42.4 28.5 all-gather.7
  72.6 150.4 all-gather.5
  226.0 50.6 all-reduce.2
  279.6 52.5 reduce-scatter.1
  333.6 151.7 all-gather.13
  487.3 50.7 all-gather.11
where the time goes:
time: 636 us; the launch traced here: 635 us
  waiting for transfers between devices  379 us (60%)
  other arithmetic  71.3 us (11%)
  blocking collectives  61.3 us (10%)
  local copies, waits for them, and re-layouts  58.8 us (9%)
  matrix products  50.1 us (8%)
  between operations  13.6 us (2%)
    all_gather x1, waiting for transfers between devices, body(): out_columns = lax.all_gather(w_out, 'fsdp', axis=1, tiled=True)  134 us
    all_gather x1, waiting for transfers between devices, body(): lax.all_gather(w_query, 'fsdp', axis=0, tiled=True)  98.2 us
    unnamed x2, other arithmetic  61.1 us
    reduce_scatter x1, waiting for transfers between devices, body(): lax.psum_scatter(query_part.astype(jnp.bfloat16), 'seq', scatter_dimensio...  53.8 us
    all_gather x1, waiting for transfers between devices, body(): lax.all_gather(heads_out, 'seq', axis=1, tiled=True)  52.6 us
    psum x1, waiting for transfers between devices, body(): lax.psum(key_part.astype(jnp.bfloat16), 'seq').astype(jnp.float32)  38.6 us
    all_to_all x1, blocking collectives, body(): lax.all_to_all(normed_input[None], 'seq', split_axis=2, concat_axis=1, ti...  31.4 us
    all_to_all x1, blocking collectives, body(): lax.all_to_all(branch[None], 'seq', split_axis=1, concat_axis=2, tiled=True)  29.9 us
  transfers between devices with their start and end apart: 7, of which 5 were waited for; matrix products, arithmetic and copies ran while one was open for 19% of the time, Pallas kernels for 0%

commit v1 on v0

--- a/solution.py
+++ b/solution.py
@@ -55,7 +55,12 @@
 
     attended = lax.map(one_head, queries)
     heads_out = jnp.transpose(attended, (1, 0, 2)).reshape(seq_length, local_heads * HEAD_SIZE)
-    out_columns = lax.all_gather(w_out, "fsdp", axis=1, tiled=True)
+    ring = [w_out]
+    for hop in range(7):
+        ring.append(lax.ppermute(ring[-1], "fsdp", [(dev, (dev + 1) % 8) for dev in range(8)]))
+    out_columns = jnp.roll(
+        jnp.concatenate(ring[::-1], axis=1), (lax.axis_index("fsdp") + 1) * ring[0].shape[1], axis=1
+    )
     mixed = jnp.dot(
         lax.all_gather(heads_out, "seq", axis=1, tiled=True),
         out_columns,

time: 636 us -> 565 us (0.89)
  waiting for transfers between devices: 379 us -> 287 us
  local copies, waits for them, and re-layouts: 58.8 us -> 104 us
  blocking collectives: 61.3 us -> 29.9 us
    ppermute x0 -> x7, waiting for transfers between devices: none -> 149 us  [body(): lax.ppermute(ring[-1], 'fsdp', [(dev, (dev + 1) % 8) for dev in range(8)])]
    all_gather x1 -> x0, waiting for transfers between devices: 134 us -> none  [body(): out_columns = lax.all_gather(w_out, 'fsdp', axis=1, tiled=True)]
    reduce_scatter x1, waiting for transfers between devices: 53.8 us -> 3.21 us  [body(): lax.psum_scatter(query_part.astype(jnp.bfloat16), 'seq', scatter_dimensio...]
    unnamed x12 -> x35, local copies, waits for them, and re-layouts: 23.8 us -> 67.2 us
    psum x1, waiting for transfers between devices: 38.6 us -> 0.01 us  [body(): lax.psum(key_part.astype(jnp.bfloat16), 'seq').astype(jnp.float32)]
    all_gather x1, waiting for transfers between devices: 52.6 us -> 16.7 us  [body(): lax.all_gather(heads_out, 'seq', axis=1, tiled=True)]
    all_to_all x1 -> x0, blocking collectives: 31.4 us -> none  [body(): lax.all_to_all(normed_input[None], 'seq', split_axis=2, concat_axis=1, ti...]
    all_to_all x0 -> x1, waiting for transfers between devices: none -> 25.3 us  [body(): lax.all_to_all(normed_input[None], 'seq', split_axis=2, concat_axis=1, ti...]
  transfers between devices with their start and end apart: 7 -> 14, of which waited for: 5 -> 9; matrix products, arithmetic and copies ran while one was open for 19% -> 26% of each run, Pallas kernels for 0% -> 0%
where the time goes in v1:
time: 565 us; the launch traced here: 563 us
  waiting for transfers between devices  287 us (51%)
  local copies, waits for them, and re-layouts  104 us (18%)
  other arithmetic  72.9 us (13%)
  matrix products  49.9 us (9%)
  blocking collectives  29.9 us (5%)
  between operations  13.6 us (2%)
  starting transfers between devices  5.89 us (1%)
    ppermute x7, waiting for transfers between devices, body(): lax.ppermute(ring[-1], 'fsdp', [(dev, (dev + 1) % 8) for dev in range(8)])  149 us
    all_gather x1, waiting for transfers between devices, body(): lax.all_gather(w_query, 'fsdp', axis=0, tiled=True)  90.8 us
    unnamed x35, local copies, waits for them, and re-layouts  67.2 us
    unnamed x2, other arithmetic  61 us
    all_to_all x1, blocking collectives, body(): lax.all_to_all(branch[None], 'seq', split_axis=1, concat_axis=2, tiled=True)  29.9 us
    all_to_all x1, waiting for transfers between devices, body(): lax.all_to_all(normed_input[None], 'seq', split_axis=2, concat_axis=1, ti...  25.3 us
    dot_general x3, matrix products, body(): jnp.dot(spread, portion, preferred_element_type=jnp.float32)  23 us
    all_gather x1, waiting for transfers between devices, body(): lax.all_gather(heads_out, 'seq', axis=1, tiled=True)  16.7 us
  transfers between devices with their start and end apart: 14, of which 9 were waited for; matrix products, arithmetic and copies ran while one was open for 26% of the time, Pallas kernels for 0%

profile of v1, /device:TPU:0, one launch (start us, length us, event | category | flops | bytes accessed | tf_op | source)
XLA Modules:
  0.0 563.4 jit_solution(5845005740164583560)
XLA Ops:
  11.4 42.9 %collective-permute-done = bf16[4096,256]{1,0:T(8,128)(2,1)} collective-permute-done((bf16[4096,256]{1,0:T(8,128)(2,1)}, bf16[4096,256]{1,0:T(8,128)(2,1)}, u32[]{:S(2)}, u32[]{:S(2)}) %collective-permute-start) | collective-permute-done | bytes 2097184 | tf_op jit(solution)/shard_map/ppermute | solution.py:60
  56.2 9.5 %copy.25 = bf16[1,128,8192]{1,0,2:T(2,128)(2,1)} copy(bf16[1,128,8192]{2,1,0:T(8,128)(2,1)} %fusion.12) | data formatting | bytes 4194304 | tf_op jit(solution)/shard_map/convert_element_type | solution.py:12
  66.3 46.5 %reduce.1 = bf16[8192,128]{1,0:T(8,128)(2,1)} reduce(bf16[8192,1,128]{2,1,0:T(2,128)(2,1)} %bitcast.51, bf16[]{:T(256)} %broadcast.28), dimensions={1}, to_apply=%bitcast.23.reduce_sub_computation | reduce | bytes 4194306
  116.8 4.5 all-to-all-start
  121.7 25.3 %all-to-all-done = bf16[4,2,131072]{2,1,0:T(2,128)(2,1)} async-done(((bf16[4,2,131072]{2,1,0:T(2,128)(2,1)}), bf16[4,2,131072]{2,1,0:T(2,128)(2,1)}, u32[]{:S(2)}, u32[]{:S(2)}) %all-to-all-start) | async-done | bytes 2097184 | tf_op jit(solution)/shard_map/all_to_all | solution.py:13
  147.0 4.9 reshape.54
  159.7 4.4 convolution_convert_fusion.2
  168.5 25.6 %collective-permute-done.2 = bf16[4096,256]{1,0:T(8,128)(2,1)} collective-permute-done((bf16[4096,256]{1,0:T(8,128)(2,1)}, bf16[4096,256]{1,0:T(8,128)(2,1)}, u32[]{:S(2)}, u32[]{:S(2)}) %collective-permute-start.2) | collective-permute-done | bytes 2097184 | tf_op jit(solution)/shard_map/ppermute | solution.py:60
  194.1 90.8 %all-gather.5.cloned.1.call-done = bf16[2048,4096]{1,0:T(8,128)(2,1)} async-done(((bf16[256,4096]{1,0:T(8,128)(2,1)}), bf16[2048,4096]{1,0:T(8,128)(2,1)}) %all-gather.5.cloned.1.call-update) | async-done | bytes 16777232 | tf_op jit(solution)/shard_map/all_gather | solution.py:22
  284.9 14.3 %convolution_convert_fusion.1 = bf16[512,4096]{1,0:T(8,128)(2,1)} fusion(bf16[512,2048]{1,0:T(8,128)(2,1)} %bitcast.59, bf16[2048,4096]{1,0:T(8,128)(2,1)} %all-gather.5.cloned.1.call-done), kind=kOutput, calls=%fused_computation.18 | convolution fusion | flops 8592031744 | bytes 23068672 | tf_op jit(solution)/shard_map/dot_general | solution.py:27
  299.6 27.2 %collective-permute-done.4 = bf16[4096,256]{1,0:T(8,128)(2,1)S(1)} collective-permute-done((bf16[4096,256]{1,0:T(8,128)(2,1)}, bf16[4096,256]{1,0:T(8,128)(2,1)S(1)}, u32[]{:S(2)}, u32[]{:S(2)}) %collective-permute-start.4) | collective-permute-done | bytes 2097184 | tf_op jit(solution)/shard_map/ppermute | solution.py:60
  328.2 27.4 %collective-permute-done.5 = bf16[4096,256]{1,0:T(8,128)(2,1)} collective-permute-done((bf16[4096,256]{1,0:T(8,128)(2,1)S(1)}, bf16[4096,256]{1,0:T(8,128)(2,1)}, u32[]{:S(2)}, u32[]{:S(2)}) %collective-permute-start.5) | collective-permute-done | bytes 2097184 | tf_op jit(solution)/shard_map/ppermute | solution.py:60
  357.2 25.9 %collective-permute-done.6 = bf16[4096,256]{1,0:T(8,128)(2,1)} collective-permute-done((bf16[4096,256]{1,0:T(8,128)(2,1)}, bf16[4096,256]{1,0:T(8,128)(2,1)}, u32[]{:S(2)}, u32[]{:S(2)}) %collective-permute-start.6) | collective-permute-done | bytes 2097184 | tf_op jit(solution)/shard_map/ppermute | solution.py:60
  396.4 16.2 %while.11 = (s32[]{:T(128)}, bf16[8,512,128]{1,2,0:T(8,128)(2,1)S(1)}, bf16[8,512,128]{2,1,0:T(8,128)(2,1)}, bf16[512,128]{1,0:T(8,128)(2,1)}, bf16[512,128]{1,0:T(8,128)(2,1)S(1)}, /*index=5*/s32[]{:T(128)}) while((s32[]{:T(128)}, bf16[8,512,128]{1,2,0:T(8,128)(2,1)S(1)}, bf16[8,512,128]{2,1,0:T(8,128)(2,1)}, ...), condition=%wide.region_7.8_spmd.clone, body=%wide.region_4.7_spmd.clone.sunk | while | flops 136641536 | bytes 4204629 | solution.py:56
  449.6 16.7 %all-gather.11.cloned.1.call-done = bf16[512,4096]{0,1:T(8,128)(2,1)} async-done(((bf16[512,1024]{0,1:T(8,128)(2,1)}), bf16[512,4096]{0,1:T(8,128)(2,1)}) %all-gather.11.cloned.1.call-update) | async-done | bytes 4194320 | tf_op jit(solution)/shard_map/all_gather | solution.py:65
  466.3 13.6 %fusion.16 = bf16[1,512,2048]{2,1,0:T(8,128)(2,1)S(1)} fusion(bf16[512,4096]{0,1:T(8,128)(2,1)} %all-gather.11.cloned.1.call-done, bf16[4096,4096]{1,0:T(8,128)(2,1)} %constant_dynamic-update-slice_fusion.1, s32[]{:T(128)S(6)} %select_n.28), kind=kOutput, calls=%fused_computation.24 | convolution fusion | flops 8590983168 | bytes 23068676 | tf_op jit(solution)/shard_map/dot_general | solution.py:64
  479.9 5.2 copy.39
  485.2 14.5 %reduce.2 = bf16[512,2048]{1,0:T(8,128)(2,1)} reduce(bf16[512,1,2048]{2,1,0:T(2,128)(2,1)} %bitcast.52, bf16[]{:T(256)} %broadcast.28), dimensions={1}, to_apply=%bitcast.42.reduce_sub_computation | reduce | bytes 4194306
  499.7 4.5 reshape.55
  504.1 29.9 %all_to_all.24 = bf16[4,2,131072]{2,1,0:T(2,128)(2,1)} all-to-all(bf16[4,2,131072]{2,1,0:T(2,128)(2,1)} %reshape.55), channel_id=1, replica_groups=mesh['seq'=4,'fsdp'=8] {'seq'}, dimensions={0} | all-to-all | bytes 4194304 | tf_op jit(solution)/shard_map/all_to_all | solution.py:70
  534.1 4.9 reshape.56
  539.0 6.8 %copy.38 = f32[1,4,128,2048]{3,1,2,0:T(4,128)} copy(bf16[1,4,128,2048]{3,0,2,1:T(2,128)(2,1)} %bitcast.54) | data formatting | bytes 6291456 | tf_op jit(solution)/shard_map/convert_element_type | solution.py:71
  545.9 6.0 %reshape.51 = f32[1,128,8192]{2,1,0:T(8,128)} reshape(f32[1,128,4,2048]{3,2,1,0:T(4,128)} %bitcast.55) | data formatting | bytes 8388608 | tf_op jit(solution)/shard_map/convert_element_type | solution.py:71
  551.9 4.6 convert_add_fusion
  (106 shorter events, 93.4 us)
Async XLA Ops:
  6.5 47.7 %copy-start = (bf16[1,128,8192]{2,1,0:T(8,128)(2,1)S(1)}, bf16[1,128,8192]{2,1,0:T(8,128)(2,1)}, u32[]{:S(2)}) copy-start(bf16[1,128,8192]{2,1,0:T(8,128)(2,1)} %param.8) | copy-start | bytes 6291460
  6.5 47.7 %copy-start.6 = (f32[8192]{0:T(1024)S(1)}, f32[8192]{0:T(1024)}, u32[]{:S(2)}) copy-start(f32[8192]{0:T(1024)} %param.9) | copy-start | bytes 98308
  6.5 153.2 %all-gather.9.cloned.1.call-start = ((), (), s32[]{:S(2)}) async-start(), calls=%async_computation.6 | async-start | bytes 2359296 | tf_op jit(solution)/shard_map/all_gather | solution.py:24
  7.3 156.9 %all-gather.7.cloned.1.call-start = ((), (), s32[]{:S(2)}) async-start(), calls=%async_computation.5 | async-start | bytes 2359296 | tf_op jit(solution)/shard_map/all_gather | solution.py:23
  8.0 276.9 %all-gather.5.cloned.1.call-start = ((), (), s32[]{:S(2)}) async-start(), calls=%async_computation.3 | async-start | bytes 18874368 | tf_op jit(solution)/shard_map/all_gather | solution.py:22
  8.7 45.5 %collective-permute-start = (bf16[4096,256]{1,0:T(8,128)(2,1)}, bf16[4096,256]{1,0:T(8,128)(2,1)}, u32[]{:S(2)}, u32[]{:S(2)}) collective-permute-start(bf16[4096,256]{1,0:T(8,128)(2,1)} %param.13), channel_id=1, source_target_pairs={{0,1},{1,2},{2,3},{3,4},{4,5},{5,6},{6,7},{7,0},{8,9},{9,10},{10,1... | collective-permute-start | bytes 6291464 | tf_op jit(solution)/shard_map/ppermute | solution.py:60
  54.3 67.0 %collective-permute-start.1 = (bf16[4096,256]{1,0:T(8,128)(2,1)}, bf16[4096,256]{1,0:T(8,128)(2,1)}, u32[]{:S(2)}, u32[]{:S(2)}) collective-permute-start(bf16[4096,256]{1,0:T(8,128)(2,1)} %collective-permute-done), channel_id=1, source_target_pairs={{0,1},{1,2},{2,3},{3,4},{4,5},{5,6},{6,7},{7,0},{8,9},{9,10},{10,1... | collective-permute-start | bytes 6291464 | tf_op jit(solution)/shard_map/ppermute | solution.py:60
  116.8 30.2 %all-to-all-start = ((bf16[4,2,131072]{2,1,0:T(2,128)(2,1)}), bf16[4,2,131072]{2,1,0:T(2,128)(2,1)}, u32[]{:S(2)}, u32[]{:S(2)}) async-start(bf16[4,2,131072]{2,1,0:T(2,128)(2,1)} %reshape.53), calls=%async_computation | async-start | bytes 4194304 | tf_op jit(solution)/shard_map/all_to_all | solution.py:13
  121.3 234.3 %all-reduce.3.cloned.1.call-start = ((), (), s32[]{:S(2)}) async-start(), calls=%async_computation.8 | async-start | bytes 2097152 | tf_op jit(solution)/shard_map/psum | solution.py:33
  121.3 72.8 %collective-permute-start.2 = (bf16[4096,256]{1,0:T(8,128)(2,1)}, bf16[4096,256]{1,0:T(8,128)(2,1)}, u32[]{:S(2)}, u32[]{:S(2)}) collective-permute-start(bf16[4096,256]{1,0:T(8,128)(2,1)} %collective-permute-done.1), channel_id=1, source_target_pairs={{0,1},{1,2},{2,3},{3,4},{4,5},{5,6},{6,7},{7,0},{8,9},{9,10},{10,1... | collective-permute-start | bytes 6291464 | tf_op jit(solution)/shard_map/ppermute | solution.py:60
  168.4 225.6 %reduce-scatter.2.cloned.1.call-start = ((), (), s32[]{:S(2)}) async-start(), calls=%async_computation.4 | async-start | bytes 5242880 | tf_op jit(solution)/shard_map/reduce_scatter | solution.py:29
  194.1 105.2 %collective-permute-start.3 = (bf16[4096,256]{1,0:T(8,128)(2,1)}, bf16[4096,256]{1,0:T(8,128)(2,1)}, u32[]{:S(2)}, u32[]{:S(2)}) collective-permute-start(bf16[4096,256]{1,0:T(8,128)(2,1)} %collective-permute-done.2), channel_id=1, source_target_pairs={{0,1},{1,2},{2,3},{3,4},{4,5},{5,6},{6,7},{7,0},{8,9},{9,10},{10,1... | collective-permute-start | bytes 6291464 | tf_op jit(solution)/shard_map/ppermute | solution.py:60
  299.3 167.0 %all-gather.11.cloned.1.call-start = ((), (), s32[]{:S(2)}) async-start(), calls=%async_computation.7 | async-start | bytes 5242880 | tf_op jit(solution)/shard_map/all_gather | solution.py:65
  299.3 27.5 %collective-permute-start.4 = (bf16[4096,256]{1,0:T(8,128)(2,1)}, bf16[4096,256]{1,0:T(8,128)(2,1)S(1)}, u32[]{:S(2)}, u32[]{:S(2)}) collective-permute-start(bf16[4096,256]{1,0:T(8,128)(2,1)} %collective-permute-done.3), channel_id=1, source_target_pairs={{0,1},{1,2},{2,3},{3,4},{4,5},{5,6},{6,7},{7,0},{8,9},{9,10},{10,1... | collective-permute-start | bytes 6291464 | tf_op jit(solution)/shard_map/ppermute | solution.py:60
  326.8 1.4 copy-start.2
  328.2 27.4 %collective-permute-start.5 = (bf16[4096,256]{1,0:T(8,128)(2,1)S(1)}, bf16[4096,256]{1,0:T(8,128)(2,1)}, u32[]{:S(2)}, u32[]{:S(2)}) collective-permute-start(bf16[4096,256]{1,0:T(8,128)(2,1)S(1)} %collective-permute-done.4), channel_id=1, source_target_pairs={{0,1},{1,2},{2,3},{3,4},{4,5},{5,6},{6,7},{7,0},{8,9},{9,10},{10,1... | collective-permute-start | bytes 6291464 | tf_op jit(solution)/shard_map/ppermute | solution.py:60
  355.6 27.6 %collective-permute-start.6 = (bf16[4096,256]{1,0:T(8,128)(2,1)}, bf16[4096,256]{1,0:T(8,128)(2,1)}, u32[]{:S(2)}, u32[]{:S(2)}) collective-permute-start(bf16[4096,256]{1,0:T(8,128)(2,1)} %collective-permute-done.5), channel_id=1, source_target_pairs={{0,1},{1,2},{2,3},{3,4},{4,5},{5,6},{6,7},{7,0},{8,9},{9,10},{10,1... | collective-permute-start | bytes 6291464 | tf_op jit(solution)/shard_map/ppermute | solution.py:60
  357.2 32.1 %copy-start.3 = (bf16[4096,256]{1,0:T(8,128)(2,1)S(1)}, bf16[4096,256]{1,0:T(8,128)(2,1)}, u32[]{:S(2)}) copy-start(bf16[4096,256]{1,0:T(8,128)(2,1)} %copy-done.2) | copy-start | bytes 6291460
  412.6 1.0 copy-start.5
  419.8 6.6 %copy-start.1 = (bf16[4096,256]{1,0:T(8,128)(2,1)S(1)}, bf16[4096,256]{1,0:T(8,128)(2,1)}, u32[]{:S(2)}) copy-start(bf16[4096,256]{1,0:T(8,128)(2,1)} %param.13) | copy-start | bytes 6291460
  427.9 6.3 %copy-start.4 = (bf16[4096,256]{1,0:T(8,128)(2,1)S(1)}, bf16[4096,256]{1,0:T(8,128)(2,1)}, u32[]{:S(2)}) copy-start(bf16[4096,256]{1,0:T(8,128)(2,1)} %copy-done.2) | copy-start | bytes 6291460
Sparse Core Ops, SparseCore 0:
  8.9 41.6 all-gather.8
  52.2 37.1 all-gather.6
  91.0 193.8 all-gather.4
  287.8 50.6 all-reduce.2
  341.4 52.5 reduce-scatter.1
  413.7 52.5 all-gather.10
